TPU v7x, 32 devices: a whole 2x2x4 slice. The times are simulated.
32 devices in a mesh: row: 8 (over y, x, core), col: 4 (over z).
Axes of the slice: x: 2, y: 2, z: 4, core: 2. Of those that a mesh axis runs over, the one named last changes fastest.
Arguments:
- gradient: float32 [2048, 4608], P('row', 'col'), may hold values from -12 to 12
- first_moment: float32 [2048, 4608], P('row', 'col'), may hold values from -12 to 12, as said below
- second_moment: float32 [2048, 4608], P('row', 'col'), may hold values from 0.01 to 1
- weights: float32 [2048, 4608], P('row', 'col'), may hold values from -6 to 6
- eigenbasis: float32 [4608, 4608], P('row', 'col'), may hold values from -1 to 1, as said below
Outputs:
- new_weights: float32 [2048, 4608], P('row', 'col')
- new_first: float32 [2048, 4608], P('row', 'col')
- new_second: float32 [2048, 4608], P('row', 'col')
Inputs may be any that keep to these rules, and one draw needn't show every extreme that they name: `first_moment`: every entry's magnitude is at most 12. eigenbasis is orthogonal: its columns are orthonormal.
All inputs are finite; a program needn't handle non-finite values.
Results may differ from a plain program's by a relative error of at most 0.000059.
Values sent between devices are 32-bit elements; how exact they have to be, the bound alone decides.
No kernel may reach another device: no remote copies, remote signals or barrier semaphores. Data moves between devices by JAX's collectives and lax.ppermute only.
A program may use at most 64 MiB of HBM per device.

v0:
```python
import jax
import jax.numpy as jnp
from jax import lax
from jax.sharding import PartitionSpec as P

D = 4608
bias_first = 1.0 - 0.9**10
bias_second = 1.0 - 0.999**10
epsilon = 1e-08
step_rate = 0.25


def per_device(gradient, first_moment, second_moment, weights, eigenbasis):
    highest = lax.Precision.HIGHEST
    slab = lax.all_gather(eigenbasis, "row", axis=0, tiled=True)
    rotated = jnp.dot(
        lax.all_gather(gradient, "col", axis=1, tiled=True),
        slab,
        precision=highest,
        preferred_element_type=jnp.float32,
    )
    new_first = 0.9 * first_moment + 0.1 * rotated
    new_second = 0.999 * second_moment + 0.001 * rotated * rotated
    direction = new_first / bias_first / (jnp.sqrt(new_second / bias_second) + epsilon)
    sum_squares = lax.psum(jnp.sum(direction * direction, axis=1), "col")
    update = lax.psum_scatter(
        lax.dot_general(
            slab,
            direction,
            (((1,), (1,)), ((), ())),
            precision=highest,
            preferred_element_type=jnp.float32,
        ),
        "col",
        scatter_dimension=0,
        tiled=True,
    ).T
    row_rms = jnp.sqrt(sum_squares / D)[:, None]
    new_weights = weights - step_rate * update / jnp.maximum(1.0, row_rms)
    return (new_weights, new_first, new_second)


def solution(mesh):
    placed = (P("row", "col"), P("row", "col"), P("row", "col"), P("row", "col"), P("row", "col"))
    return jax.shard_map(
        per_device,
        mesh=mesh,
        in_specs=placed,
        out_specs=(P("row", "col"), P("row", "col"), P("row", "col")),
        check_vma=False,
    )
```

profile of v0, /device:TPU:0, one launch (start us, length us, event | category | flops | bytes accessed | tf_op | source)
XLA Modules:
  0.0 354.3 jit_solution(7112353394276214522)
XLA Ops:
  7.2 0.0 all-gather.3.cloned.1.call-start
  7.2 0.7 all-gather.3.cloned.1.call-update
  7.9 0.0 copy-start.3
  7.9 0.0 all-gather.5.cloned.1.call-start
  8.0 0.7 all-gather.5.cloned.1.call-update
  8.7 0.0 reduce-scatter.2.cloned.1.call-start
  8.7 93.0 %all-gather.3.cloned.1.call-done = f32[256,4608]{1,0:T(8,128)} async-done(((f32[256,1152]{1,0:T(8,128)}), f32[256,4608]{1,0:T(8,128)}) %all-gather.3.cloned.1.call-update) | async-done | bytes 4718608 | tf_op jit(solution)/shard_map/all_gather | solution.py:17
  101.7 108.9 %all-gather.5.cloned.1.call-done = f32[4608,1152]{1,0:T(8,128)} async-done(((f32[576,1152]{1,0:T(8,128)}), f32[4608,1152]{1,0:T(8,128)}) %all-gather.5.cloned.1.call-update) | async-done | bytes 21233680 | tf_op jit(solution)/shard_map/all_gather | solution.py:15
  210.6 0.0 copy-done.3
  210.6 0.0 copy-start
  210.6 26.6 %multiply_reduce_fusion = (f32[256]{0:T(256)S(1)}, f32[256,1152]{1,0:T(8,128)S(1)}, f32[256,1152]{1,0:T(8,128)S(1)}) fusion(f32[256,1152]{1,0:T(8,128)S(1)} %copy-done.3, f32[256,1152]{1,0:T(8,128)} %param.7, f32[256,4608]{1,0:T(8,128)} %all-gather.3.cloned.1.call-done, f32[4608,1152]{1,0:T(8,128)} %all-gather.5.cloned.1.call-done), kind=kOutput, calls=%fused_computation.4 | convolution fusion | flops 16311287808 | bytes 30671872 | tf_op jit(solution)/shard_map/dot_general | solution.py:16
  237.2 0.0 copy-start.1
  237.3 0.0 copy-start.2
  237.3 0.0 copy-done
  237.3 22.5 %convolution_bitcast_fusion = f32[4608,256]{0,1:T(8,128)} fusion(f32[4608,1152]{1,0:T(8,128)S(1)} %copy-done, f32[256,1152]{1,0:T(8,128)S(1)} %get-tuple-element.5, f32[256,1152]{1,0:T(8,128)S(1)} %get-tuple-element.4), kind=kOutput, calls=%fused_computation | convolution fusion | flops 16308633600 | bytes 28311552 | tf_op jit(solution)/shard_map/dot_general | solution.py:27
  259.8 0.0 copy-done.1
  259.8 0.0 copy-done.2
  259.8 0.0 copy-start.4
  259.8 0.0 reduce-scatter.2.cloned.1.call-update
  259.8 12.1 %psum.7 = f32[256]{0:T(256)S(1)} all-reduce(f32[256]{0:T(256)S(1)} %get-tuple-element.3), channel_id=1, replica_groups=mesh['row'=8,'col'=4] {'col'}, use_global_device_ids=true, to_apply=%region_2.0 | all-reduce | flops 256 | bytes 2048 | tf_op jit(solution)/shard_map/psum | solution.py:25
  271.9 73.4 %reduce-scatter.2.cloned.1.call-done = f32[1152,256]{0,1:T(8,128)} async-done(((f32[4608,256]{0,1:T(8,128)}), f32[1152,256]{0,1:T(8,128)}) %reduce-scatter.2.cloned.1.call-update) | async-done | bytes 1179664 | tf_op jit(solution)/shard_map/reduce_scatter | solution.py:26
  345.3 0.0 copy-done.4
  345.3 2.5 bitcast_subtract_fusion
  (1 shorter events, 0.0 us)
Async XLA Ops:
  7.2 94.5 %all-gather.3.cloned.1.call-start = ((), (), s32[]{:S(2)}) async-start(), calls=%async_computation.1 | async-start | bytes 5898240 | tf_op jit(solution)/shard_map/all_gather | solution.py:17
  7.9 202.7 %copy-start.3 = (f32[256,1152]{1,0:T(8,128)S(1)}, f32[256,1152]{1,0:T(8,128)}, u32[]{:S(2)}) copy-start(f32[256,1152]{1,0:T(8,128)} %param.6) | copy-start | bytes 3538948
  7.9 202.7 %all-gather.5.cloned.1.call-start = ((), (), s32[]{:S(2)}) async-start(), calls=%async_computation.2 | async-start | bytes 23887872 | tf_op jit(solution)/shard_map/all_gather | solution.py:15
  8.7 336.7 %reduce-scatter.2.cloned.1.call-start = ((), (), s32[]{:S(2)}) async-start(), calls=%async_computation.3 | async-start | bytes 5898240 | tf_op jit(solution)/shard_map/reduce_scatter | solution.py:26
  210.6 26.7 %copy-start = (f32[4608,1152]{1,0:T(8,128)S(1)}, f32[4608,1152]{1,0:T(8,128)}, u32[]{:S(2)}) copy-start(f32[4608,1152]{1,0:T(8,128)} %all-gather.5.cloned.1.call-done) | copy-start | bytes 63700996
  237.2 22.5 %copy-start.1 = (f32[256,1152]{1,0:T(8,128)}, f32[256,1152]{1,0:T(8,128)S(1)}, u32[]{:S(2)}) copy-start(f32[256,1152]{1,0:T(8,128)S(1)} %get-tuple-element.4) | copy-start | bytes 3538948
  237.3 22.5 %copy-start.2 = (f32[256,1152]{1,0:T(8,128)}, f32[256,1152]{1,0:T(8,128)S(1)}, u32[]{:S(2)}) copy-start(f32[256,1152]{1,0:T(8,128)S(1)} %get-tuple-element.5) | copy-start | bytes 3538948
  259.8 85.5 %copy-start.4 = (f32[256,1152]{1,0:T(8,128)S(1)}, f32[256,1152]{1,0:T(8,128)}, u32[]{:S(2)}) copy-start(f32[256,1152]{1,0:T(8,128)} %param.8) | copy-start | bytes 3538948
Sparse Core Ops, SparseCore 0:
  9.5 92.0 all-gather.2
  103.6 106.9 all-gather.4
  259.9 85.3 reduce-scatter.1
where the time goes:
time: 355 us; the launch traced here: 354 us
  waiting for transfers between devices  277 us (78%)
  matrix products  49.1 us (14%)
  between operations  13.8 us (4%)
  blocking collectives  12.1 us (3%)
    all_gather x1, waiting for transfers between devices, per_device(): slab = lax.all_gather(eigenbasis, 'row', axis=0, tiled=True)  109 us
    all_gather x1, waiting for transfers between devices, per_device(): lax.all_gather(gradient, 'col', axis=1, tiled=True)  93 us
    reduce_scatter x1, waiting for transfers between devices, per_device(): lax.psum_scatter(lax.dot_general(slab, direction, (((1,), (1,)), ((), ())...  73.4 us
    dot_general x1, matrix products, per_device(): jnp.dot(lax.all_gather(gradient, 'col', axis=1, tiled=True), slab, precis...  26.6 us
    dot_general x1, matrix products, per_device(): lax.dot_general(slab, direction, (((1,), (1,)), ((), ())), precision=high...  22.5 us
    psum x1, blocking collectives, per_device(): sum_squares = lax.psum(jnp.sum(direction * direction, axis=1), 'col')  12.1 us
  transfers between devices with their start and end apart: 3, of which 3 were waited for; matrix products, arithmetic and copies ran while one was open for 0% of the time, Pallas kernels for 0%

commit v1 on v0

--- a/solution.py
+++ b/solution.py
@@ -1,3 +1,4 @@
+import functools
 import jax
 import jax.numpy as jnp
 from jax import lax
@@ -10,14 +11,34 @@
 step_rate = 0.25
 
 
+def recast_body(original, peer_axis):
+    built, all_values, frame_out = (
+        jax.lax.psum(1, peer_axis),
+        jax.lax.axis_index(peer_axis),
+        original.shape[1],
+    )
+    ledger = [c * built if t == 1 else c for t, c in enumerate(original.shape)]
+    moved = lax.dynamic_update_slice_in_dim(
+        jnp.zeros(ledger, original.dtype), original, all_values * frame_out, axis=1
+    )
+    for k in tuple(range(1, built)):
+        original = jax.lax.ppermute(
+            original, peer_axis, [(t, (t + 1) % built) for t in range(built)]
+        )
+        moved = lax.dynamic_update_slice_in_dim(
+            moved, original, (all_values - k) % built * frame_out, axis=1
+        )
+    return moved
+
+
+local_data_number = functools.partial(recast_body, peer_axis="col")
+
+
 def per_device(gradient, first_moment, second_moment, weights, eigenbasis):
     highest = lax.Precision.HIGHEST
     slab = lax.all_gather(eigenbasis, "row", axis=0, tiled=True)
     rotated = jnp.dot(
-        lax.all_gather(gradient, "col", axis=1, tiled=True),
-        slab,
-        precision=highest,
-        preferred_element_type=jnp.float32,
+        local_data_number(gradient), slab, precision=highest, preferred_element_type=jnp.float32
     )
     new_first = 0.9 * first_moment + 0.1 * rotated
     new_second = 0.999 * second_moment + 0.001 * rotated * rotated

time: 355 us -> 266 us (0.75)
  waiting for transfers between devices: 277 us -> 174 us
  local copies, waits for them, and re-layouts: 0.03 us -> 10.3 us
    all_gather x1 -> x0, waiting for transfers between devices: 93 us -> none  [per_device(): lax.all_gather(gradient, 'col', axis=1, tiled=True)]
    all_gather x1, waiting for transfers between devices: 109 us -> 21.9 us  [per_device(): slab = lax.all_gather(eigenbasis, 'row', axis=0, tiled=True)]
    ppermute x0 -> x3, waiting for transfers between devices: none -> 78.1 us  [recast_body(): jax.lax.ppermute(original, peer_axis, [(t, (t + 1) % built) for t in rang...]
    dynamic_update_slice x0 -> x4, local copies, waits for them, and re-layouts: none -> 7.05 us  [the longest x3 5.93 us: recast_body(): lax.dynamic_update_slice_in_dim(moved, original, (all_values - k) % built...]
  transfers between devices with their start and end apart: 3 -> 5, of which waited for: 3 -> 5; matrix products, arithmetic and copies ran while one was open for 0% -> 4% of each run, Pallas kernels for 0% -> 0%
where the time goes in v1:
time: 266 us; the launch traced here: 265 us
  waiting for transfers between devices  174 us (65%)
  matrix products  49.1 us (18%)
  between operations  14.1 us (5%)
  blocking collectives  12.1 us (5%)
  local copies, waits for them, and re-layouts  10.3 us (4%)
  starting transfers between devices  3.13 us (1%)
    ppermute x3, waiting for transfers between devices, recast_body(): jax.lax.ppermute(original, peer_axis, [(t, (t + 1) % built) for t in rang...  78.1 us
    reduce_scatter x1, waiting for transfers between devices, per_device(): lax.psum_scatter(lax.dot_general(slab, direction, (((1,), (1,)), ((), ())...  73.5 us
    dot_general x1, matrix products, per_device(): jnp.dot(local_data_number(gradient), slab, precision=highest, preferred_e...  26.7 us
    dot_general x1, matrix products, per_device(): lax.dot_general(slab, direction, (((1,), (1,)), ((), ())), precision=high...  22.4 us
    all_gather x1, waiting for transfers between devices, per_device(): slab = lax.all_gather(eigenbasis, 'row', axis=0, tiled=True)  21.9 us
    psum x1, blocking collectives, per_device(): sum_squares = lax.psum(jnp.sum(direction * direction, axis=1), 'col')  12.1 us
    dynamic_update_slice x3, local copies, waits for them, and re-layouts, recast_body(): lax.dynamic_update_slice_in_dim(moved, original, (all_values - k) % built...  5.93 us
  transfers between devices with their start and end apart: 5, of which 5 were waited for; matrix products, arithmetic and copies ran while one was open for 4% of the time, Pallas kernels for 0%

profile of v1, /device:TPU:0, one launch (start us, length us, event | category | flops | bytes accessed | tf_op | source)
XLA Modules:
  0.0 265.3 jit_solution(10869952306759583699)
XLA Ops:
  7.2 0.0 all-gather.2.cloned.1.call-start
  7.2 0.7 all-gather.2.cloned.1.call-update
  7.9 0.0 reduce-scatter.2.cloned.1.call-start
  8.0 0.5 copy-done.4
  8.4 3.1 %collective-permute-start = (f32[256,1152]{1,0:T(8,128)S(1)}, f32[256,1152]{1,0:T(8,128)S(1)}, u32[]{:S(2)}, u32[]{:S(2)}) collective-permute-start(f32[256,1152]{1,0:T(8,128)S(1)} %copy-done.4), channel_id=1, source_target_pairs={{0,1},{1,2},{2,3},{3,0},{4,5},{5,6},{6,7},{7,4},{8,9},{9,10},{10,1... | collective-permute-start | bytes 3538952 | tf_op jit(solution)/shard_map/ppermute | solution.py:25
  11.5 28.0 %collective-permute-done = f32[256,1152]{1,0:T(8,128)S(1)} collective-permute-done((f32[256,1152]{1,0:T(8,128)S(1)}, f32[256,1152]{1,0:T(8,128)S(1)}, u32[]{:S(2)}, u32[]{:S(2)}) %collective-permute-start) | collective-permute-done | bytes 1179680 | tf_op jit(solution)/shard_map/ppermute | solution.py:25
  39.5 0.0 collective-permute-start.1
  39.5 29.0 %collective-permute-done.1 = f32[256,1152]{1,0:T(8,128)} collective-permute-done((f32[256,1152]{1,0:T(8,128)S(1)}, f32[256,1152]{1,0:T(8,128)}, u32[]{:S(2)}, u32[]{:S(2)}) %collective-permute-start.1) | collective-permute-done | bytes 1179680 | tf_op jit(solution)/shard_map/ppermute | solution.py:25
  68.5 0.0 collective-permute-start.2
  68.5 2.7 %broadcast_in_dim.4 = f32[256,4608]{1,0:T(8,128)} broadcast(f32[]{:T(128)} %constant.46.clone.1), dimensions={} | broadcast | bytes 4718596 | tf_op jit(solution)/shard_map/broadcast_in_dim | solution.py:22
  71.2 1.1 constant_dynamic-update-slice_fusion.3
  72.4 1.1 constant_dynamic-update-slice_fusion.2
  73.5 2.4 constant_dynamic-update-slice_fusion.1
  75.9 21.0 %collective-permute-done.2 = f32[256,1152]{1,0:T(8,128)} collective-permute-done((f32[256,1152]{1,0:T(8,128)}, f32[256,1152]{1,0:T(8,128)}, u32[]{:S(2)}, u32[]{:S(2)}) %collective-permute-start.2) | collective-permute-done | bytes 1179680 | tf_op jit(solution)/shard_map/ppermute | solution.py:25
  96.9 2.4 constant_dynamic-update-slice_fusion
  99.3 21.9 %all-gather.2.cloned.1.call-done = f32[4608,1152]{1,0:T(8,128)} async-done(((f32[576,1152]{1,0:T(8,128)}), f32[4608,1152]{1,0:T(8,128)}) %all-gather.2.cloned.1.call-update) | async-done | bytes 21233680 | tf_op jit(solution)/shard_map/all_gather | solution.py:39
  121.2 26.7 %multiply_reduce_fusion = (f32[256]{0:T(256)S(1)}, f32[256,1152]{1,0:T(8,128)S(1)}, f32[256,1152]{1,0:T(8,128)S(1)}) fusion(f32[256,1152]{1,0:T(8,128)S(1)} %copy-done.3, f32[256,1152]{1,0:T(8,128)} %param.7, f32[256,4608]{1,0:T(8,128)} %constant_dynamic-update-slice_fusion, f32[4608,1152]{1,0:T(8,128)} %all-gather.2.cloned.1.call-done), kind=kOutput, calls=%fused_computation.4 | convolution fusion | flops 16311287808 | bytes 30671872 | tf_op jit(solution)/shard_map/dot_general | solution.py:40
  147.9 0.0 copy-start.1
  147.9 0.0 copy-start.2
  148.0 22.4 %convolution_bitcast_fusion = f32[4608,256]{0,1:T(8,128)} fusion(f32[4608,1152]{1,0:T(8,128)S(1)} %copy-done, f32[256,1152]{1,0:T(8,128)S(1)} %get-tuple-element.5, f32[256,1152]{1,0:T(8,128)S(1)} %get-tuple-element.4), kind=kOutput, calls=%fused_computation | convolution fusion | flops 16308633600 | bytes 28311552 | tf_op jit(solution)/shard_map/dot_general | solution.py:48
  170.4 0.0 reduce-scatter.2.cloned.1.call-update
  170.4 12.1 %psum.7 = f32[256]{0:T(256)S(1)} all-reduce(f32[256]{0:T(256)S(1)} %get-tuple-element.3), channel_id=1, replica_groups=mesh['row'=8,'col'=4] {'col'}, use_global_device_ids=true, to_apply=%region_2.3 | all-reduce | flops 256 | bytes 2048 | tf_op jit(solution)/shard_map/psum | solution.py:46
  182.5 73.5 %reduce-scatter.2.cloned.1.call-done = f32[1152,256]{0,1:T(8,128)} async-done(((f32[4608,256]{0,1:T(8,128)}), f32[1152,256]{0,1:T(8,128)}) %reduce-scatter.2.cloned.1.call-update) | async-done | bytes 1179664 | tf_op jit(solution)/shard_map/reduce_scatter | solution.py:47
  256.0 2.5 bitcast_subtract_fusion
  (10 shorter events, 0.0 us)
Async XLA Ops:
  7.2 1.3 copy-start.4
  7.2 114.0 %all-gather.2.cloned.1.call-start = ((), (), s32[]{:S(2)}) async-start(), calls=%async_computation.1 | async-start | bytes 23887872 | tf_op jit(solution)/shard_map/all_gather | solution.py:39
  7.9 248.0 %reduce-scatter.2.cloned.1.call-start = ((), (), s32[]{:S(2)}) async-start(), calls=%async_computation.2 | async-start | bytes 5898240 | tf_op jit(solution)/shard_map/reduce_scatter | solution.py:47
  8.4 31.0 %collective-permute-start = (f32[256,1152]{1,0:T(8,128)S(1)}, f32[256,1152]{1,0:T(8,128)S(1)}, u32[]{:S(2)}, u32[]{:S(2)}) collective-permute-start(f32[256,1152]{1,0:T(8,128)S(1)} %copy-done.4), channel_id=1, source_target_pairs={{0,1},{1,2},{2,3},{3,0},{4,5},{5,6},{6,7},{7,4},{8,9},{9,10},{10,1... | collective-permute-start | bytes 3538952 | tf_op jit(solution)/shard_map/ppermute | solution.py:25
  39.5 29.0 %collective-permute-start.1 = (f32[256,1152]{1,0:T(8,128)S(1)}, f32[256,1152]{1,0:T(8,128)}, u32[]{:S(2)}, u32[]{:S(2)}) collective-permute-start(f32[256,1152]{1,0:T(8,128)S(1)} %collective-permute-done), channel_id=1, source_target_pairs={{0,1},{1,2},{2,3},{3,0},{4,5},{5,6},{6,7},{7,4},{8,9},{9,10},{10,1... | collective-permute-start | bytes 3538952 | tf_op jit(solution)/shard_map/ppermute | solution.py:25
  68.5 28.4 %collective-permute-start.2 = (f32[256,1152]{1,0:T(8,128)}, f32[256,1152]{1,0:T(8,128)}, u32[]{:S(2)}, u32[]{:S(2)}) collective-permute-start(f32[256,1152]{1,0:T(8,128)} %collective-permute-done.1), channel_id=1, source_target_pairs={{0,1},{1,2},{2,3},{3,0},{4,5},{5,6},{6,7},{7,4},{8,9},{9,10},{10,1... | collective-permute-start | bytes 3538952 | tf_op jit(solution)/shard_map/ppermute | solution.py:25
  75.9 45.3 %copy-start.3 = (f32[256,1152]{1,0:T(8,128)S(1)}, f32[256,1152]{1,0:T(8,128)}, u32[]{:S(2)}) copy-start(f32[256,1152]{1,0:T(8,128)} %param.6) | copy-start | bytes 3538948
  121.2 26.8 %copy-start = (f32[4608,1152]{1,0:T(8,128)S(1)}, f32[4608,1152]{1,0:T(8,128)}, u32[]{:S(2)}) copy-start(f32[4608,1152]{1,0:T(8,128)} %all-gather.2.cloned.1.call-done) | copy-start | bytes 63700996
  147.9 22.5 %copy-start.1 = (f32[256,1152]{1,0:T(8,128)}, f32[256,1152]{1,0:T(8,128)S(1)}, u32[]{:S(2)}) copy-start(f32[256,1152]{1,0:T(8,128)S(1)} %get-tuple-element.4) | copy-start | bytes 3538948
  147.9 22.4 %copy-start.2 = (f32[256,1152]{1,0:T(8,128)}, f32[256,1152]{1,0:T(8,128)S(1)}, u32[]{:S(2)}) copy-start(f32[256,1152]{1,0:T(8,128)S(1)} %get-tuple-element.5) | copy-start | bytes 3538948
  170.4 85.6 %copy-start.5 = (f32[256,1152]{1,0:T(8,128)S(1)}, f32[256,1152]{1,0:T(8,128)}, u32[]{:S(2)}) copy-start(f32[256,1152]{1,0:T(8,128)} %param.8) | copy-start | bytes 3538948
Sparse Core Ops, SparseCore 0:
  9.9 111.2 all-gather.1
  170.5 85.3 reduce-scatter.1
